TPU v7x, 512 devices: a 8x2x16 block of a 8x8x16 slice. The times are simulated.
512 devices in a mesh: groups: 2 (over y), seq: 16 (over z), head: 8 (over x), rep: 2 (over core).
Axes of the slice: x: 8, y: 2, z: 16, core: 2. Of those that a mesh axis runs over, the one named last changes fastest.
The devices are a block of a 8x8x16 slice.
Arguments:
- q_latent: bfloat16 [32, 2, 128, 512], P('groups', None, 'head'), parts along dimension 0, may hold values from -40 to 40
- q_rope: bfloat16 [32, 2, 128, 64], P('groups', None, 'head'), parts along dimension 0, may hold values from -40 to 40
- cache_latent: bfloat16 [32, 2048, 512], P(('groups', 'rep'), 'seq'), parts along dimension 0, may hold values from -20 to 20
- rope_keys: bfloat16 [32, 64, 2048], P(('groups', 'rep'), None, 'seq'), parts along dimension 0, may hold values from -20 to 20
- lengths: int32 [32], P(('groups', 'rep')), parts along dimension 0, may hold values from 128 to 2048, as said below
- slot_request: int32 [32], P(('groups', 'rep')), parts along dimension 0, may hold values from 0 to 15, as said below
- value_up: bfloat16 [128, 512, 128], P('head'), may hold values from -0.25 to 0.25
Outputs:
- values: bfloat16 [32, 2, 128, 128], P(('groups', 'rep'), None, 'head'), parts along dimension 0
There are 2 independent parts, one for each index of `groups`. A program takes and returns all parts, laid end to end along the dimension named above; an argument that names none is the same for every part. Nothing has to cross between parts.
Inputs may be any that keep to these rules, and one draw needn't show every extreme that they name: `lengths`: each slot's length lies between 128 and 2048; in every part some slot holds 2048. `slot_request`: a permutation of the requests 0 to 15.
All inputs are finite; a program needn't handle non-finite values.
Results may differ from a plain program's by a relative error of at most 0.0021.
Values may be sent and summed in bfloat16 or wider, within the bound.
No kernel may reach another device: no remote copies, remote signals or barrier semaphores. Data moves between devices by JAX's collectives and lax.ppermute only.
A program may use at most 64 MiB of HBM per device.

v0:
```python
import jax
import jax.numpy as jnp
from jax import lax
from jax.sharding import PartitionSpec as P

ROPE = 64
NOPE = 128


negative_fill = -1e30


def from_everyone(shard, axis):
    copies = jnp.broadcast_to(shard, (lax.axis_size(axis), *shard.shape))
    return lax.all_to_all(copies, axis, split_axis=0, concat_axis=0, tiled=True)


def of_everyone(shard, axis):
    return from_everyone(shard, axis).max(axis=0)


def cut_along(shard, dim, devices):
    before, after = (shard.shape[:dim], shard.shape[dim + 1 :])
    return jnp.moveaxis(shard.reshape(*before, devices, -1, *after), dim, 0)


def summed_on_arrival(shard, axis, dim):
    devices = lax.axis_size(axis)
    tiles = lax.all_to_all(cut_along(shard, dim, devices), axis, 0, 0, tiled=True)
    return jnp.sum(tiles, axis=0)


def in_one_piece(arrays, axis, dim, along):
    columns = [a.reshape(*a.shape[:along], -1) for a in arrays]
    both = jnp.concatenate(columns, axis=along)
    whole, at, finished = (summed_on_arrival(both, axis, dim), 0, [])
    for a, column in zip(arrays, columns):
        piece = whole[..., at : at + column.shape[along]]
        finished.append(piece.reshape(*piece.shape[:along], *a.shape[along:]))
        at += column.shape[along]
    return tuple(finished)


def in_order(tiles, dim):
    tiles = jnp.moveaxis(tiles, 0, dim)
    lengths = tiles.shape
    return tiles.reshape(*lengths[:dim], lengths[dim] * lengths[dim + 1], *lengths[dim + 2 :])


def gather_directly(shard, axis, dim):
    tiles = from_everyone(shard, axis)
    return in_order(tiles, dim)


def project(partial_value, weight):
    return jnp.einsum(
        "rthd,hdv->rthv", partial_value, weight.astype(jnp.float32), precision=lax.Precision.HIGHEST
    )


def per_device(q_latent, q_rope, cache_latent, rope_keys, lengths, slot_request, value_up):
    softmax_scale = (NOPE + ROPE) ** (-0.5)
    page_len = cache_latent.shape[1]
    new_tokens = q_latent.shape[1]
    query_lat = jnp.take(q_latent, slot_request, axis=0)
    query_rot = jnp.take(q_rope, slot_request, axis=0)
    scores = jnp.einsum(
        "rthd,rpd->rthp", query_lat, cache_latent, preferred_element_type=jnp.float32
    )
    scores = scores + jnp.einsum(
        "rthe,rep->rthp", query_rot, rope_keys, preferred_element_type=jnp.float32
    )
    scores = scores * softmax_scale
    positions = lax.axis_index("seq") * page_len + jnp.arange(page_len, dtype=jnp.int32)
    limits = lengths[:, None] - new_tokens + 1 + jnp.arange(new_tokens, dtype=jnp.int32)[None, :]
    visible = (positions[None, None, :] < limits[:, :, None])[:, :, None, :]
    masked = jnp.where(visible, scores, negative_fill)
    page_max = jnp.max(masked, axis=3)
    page_exp = jnp.where(visible, jnp.exp(masked - page_max[..., None]), 0.0)
    page_den = jnp.sum(page_exp, axis=3)
    page_out = jnp.einsum(
        "rthp,rpd->rthd",
        page_exp.astype(jnp.bfloat16),
        cache_latent,
        preferred_element_type=jnp.float32,
    )
    carried = project(page_out, value_up)
    largest = of_everyone(page_max, "seq")
    factor = jnp.exp(page_max - largest)
    denominator, summed = in_one_piece(
        (factor * page_den, factor[..., None] * carried), "seq", 2, 3
    )
    attended = summed / denominator[..., None]
    finished = attended.astype(jnp.bfloat16)
    return gather_directly(finished, "seq", 2)


def solution(mesh):
    in_specs = (
        P("groups", None, "head", None),
        P("groups", None, "head", None),
        P(("groups", "rep"), "seq", None),
        P(("groups", "rep"), None, "seq"),
        P(("groups", "rep")),
        P(("groups", "rep")),
        P("head", None, None),
    )
    out_specs = P(("groups", "rep"), None, "head", None)
    return jax.shard_map(
        per_device, mesh=mesh, in_specs=in_specs, out_specs=out_specs, check_vma=False
    )
```

profile of v0, /device:TPU:80, one launch (start us, length us, event | category | flops | bytes accessed | tf_op | source)
XLA Modules:
  0.0 108.4 jit_solution(13733592538029588090)
XLA Ops:
  0.0 0.0 copy-start
  0.0 0.0 copy-start.1
  0.0 0.8 compare_select_fusion
  0.8 0.7 compare_and_fusion
  1.5 1.6 %gather_fusion = bf16[8,2,16,512]{3,2,1,0:T(8,128)(2,1)S(1)} fusion(bf16[16,2,16,512]{3,2,1,0:T(8,128)(2,1)} %param.7, s32[1024]{0:T(1024)S(1)} %pad_clamp_fusion), kind=kCustom, calls=%fused_computation | custom fusion | bytes 524320 | tf_op jit(solution)/shard_map/jit(_take)/gather | solution.py:65
  3.2 1.5 %gather_fusion.1 = bf16[8,2,16,64]{3,2,1,0:T(8,128)(2,1)S(1)} fusion(bf16[16,2,16,64]{3,2,1,0:T(8,128)(2,1)} %param.8, s32[1024]{0:T(1024)S(1)} %pad_clamp_fusion), kind=kCustom, calls=%fused_computation.1 | custom fusion | bytes 65568 | tf_op jit(solution)/shard_map/jit(_take)/gather | solution.py:66
  4.6 0.7 broadcast_add_fusion
  5.3 0.1 iota_add_fusion
  5.4 0.1 broadcast_compare_fusion
  5.4 1.7 %fusion.12 = f32[8,2,16,128]{3,2,1,0:T(8,128)S(1)} fusion(bf16[8,128,512]{2,1,0:T(8,128)(2,1)} %param.9, bf16[8,2,16,512]{3,2,1,0:T(8,128)(2,1)S(1)} %gather_fusion, pred[8]{0:T(512)(128)(4,1)S(1)} %compare_and_fusion), kind=kOutput, calls=%fused_computation.11 | convolution fusion | flops 33685504 | bytes 1441800 | tf_op jit(solution)/shard_map/rthd,rpd->rthp/dot_general | solution.py:67
  7.2 1.2 %fusion.34 = (f32[8,2,16]{2,1,0:T(2,128)S(1)}, f32[8,2,16,128]{3,2,1,0:T(8,128)S(1)}) fusion(f32[8,2,16,128]{3,2,1,0:T(8,128)S(1)} %fusion.12, bf16[8,64,128]{2,1,0:T(8,128)(2,1)} %param.10, bf16[8,2,16,64]{3,2,1,0:T(8,128)(2,1)S(1)} %gather_fusion.1, pred[8]{0:T(512)(128)(4,1)S(1)} %compare_and_fusion, pred[8,2,128]{2,1,0:T(4,128)(4,1)S(1)} %broadcast_compare_fusion), kind=kOutput, calls=%fused_computation.46 | convolution fusion | flops 4341504 | bytes 429064 | tf_op jit(solution)/shard_map/rthe,rep->rthp/dot_general | solution.py:70
  8.4 0.7 reshape.97
  9.1 43.7 %all-to-all-start = ((f32[16,1,256]{2,1,0:T(1,128)}), f32[16,1,256]{2,1,0:T(1,128)S(1)}, u32[]{:S(2)}, u32[]{:S(2)}) async-start(f32[16,1,256]{2,1,0:T(1,128)} %reshape.97), calls=%async_computation | async-start | bytes 32768 | tf_op jit(solution)/shard_map/all_to_all | solution.py:15
  52.8 0.0 copy-done.1
  52.8 1.1 %fusion.10 = f32[8,2,16,512]{3,2,1,0:T(8,128)} fusion(bf16[8,128,512]{2,1,0:T(8,128)(2,1)S(1)} %copy-done.1, f32[8,2,16,128]{3,2,1,0:T(8,128)S(1)} %get-tuple-element.8, f32[8,2,16]{2,1,0:T(2,128)S(1)} %get-tuple-element.7, pred[8,2,128]{2,1,0:T(4,128)(4,1)S(1)} %broadcast_compare_fusion), kind=kOutput, calls=%fused_computation.9 | convolution fusion | flops 33652736 | bytes 1707008 | tf_op jit(solution)/shard_map/rthp,rpd->rthd/dot_general | solution.py:81
  54.0 0.2 fusion.20
  54.2 11.0 %all-to-all-done = f32[16,1,256]{2,1,0:T(1,128)S(1)} async-done(((f32[16,1,256]{2,1,0:T(1,128)}), f32[16,1,256]{2,1,0:T(1,128)S(1)}, u32[]{:S(2)}, u32[]{:S(2)}) %all-to-all-start) | async-done | bytes 16416 | tf_op jit(solution)/shard_map/all_to_all | solution.py:15
  65.1 0.5 broadcast.61
  65.6 0.7 reduce.3
  66.3 0.1 reshape.98
  66.5 0.1 copy.45
  66.6 0.2 copy.47
  66.7 0.0 copy-done
  66.7 2.2 %fusion.5 = f32[8,2,16,128]{3,0,1,2:T(8,128)S(1)} fusion(bf16[16,512,128]{2,1,0:T(8,128)(2,1)S(1)} %copy-done, f32[8,2,16,512]{3,2,1,0:T(8,128)} %fusion.10, f32[8,2,16]{0,1,2:T(2,128)S(1)} %copy.45), kind=kOutput, calls=%fused_computation.5 | convolution fusion | flops 201359360 | bytes 2753536 | tf_op jit(solution)/shard_map/rthd,hdv->rthv/dot_general | solution.py:56
  68.9 0.1 maximum_bitcast_fusion
  69.1 20.0 %all_to_all.15 = f32[16,8,2,1,129]{4,1,2,3,0:T(8,128)S(1)} all-to-all(f32[16,8,2,1,129]{4,1,2,3,0:T(8,128)S(1)} %maximum_bitcast_fusion), channel_id=1, replica_groups=mesh['groups'=2,'seq'=16,'head'=8,'rep'=2] {'seq'}, dimensions={0} | all-to-all | bytes 264192 | tf_op jit(solution)/shard_map/all_to_all | solution.py:29
  89.1 0.1 slice_reduce_fusion
  89.2 0.1 fusion.30
  89.3 18.4 %all_to_all.16 = bf16[16,8,2,1,128]{4,2,1,3,0:T(2,128)(2,1)S(1)} all-to-all(bf16[16,8,2,1,128]{4,2,1,3,0:T(2,128)(2,1)S(1)} %broadcast_in_dim.62), channel_id=1, replica_groups=mesh['groups'=2,'seq'=16,'head'=8,'rep'=2] {'seq'}, dimensions={0} | all-to-all | bytes 131072 | tf_op jit(solution)/shard_map/all_to_all | solution.py:15
  107.7 0.6 copy.51
  (9 shorter events, 0.1 us)
Async XLA Ops:
  0.0 66.7 %copy-start = (bf16[16,512,128]{2,1,0:T(8,128)(2,1)S(1)}, bf16[16,512,128]{2,1,0:T(8,128)(2,1)}, u32[]{:S(2)}) copy-start(bf16[16,512,128]{2,1,0:T(8,128)(2,1)} %param.13) | copy-start | bytes 6291460
  0.0 52.8 %copy-start.1 = (bf16[8,128,512]{2,1,0:T(8,128)(2,1)S(1)}, bf16[8,128,512]{2,1,0:T(8,128)(2,1)}, u32[]{:S(2)}) copy-start(bf16[8,128,512]{2,1,0:T(8,128)(2,1)} %param.9) | copy-start | bytes 3145732
  9.1 56.0 %all-to-all-start = ((f32[16,1,256]{2,1,0:T(1,128)}), f32[16,1,256]{2,1,0:T(1,128)S(1)}, u32[]{:S(2)}, u32[]{:S(2)}) async-start(f32[16,1,256]{2,1,0:T(1,128)} %reshape.97), calls=%async_computation | async-start | bytes 32768 | tf_op jit(solution)/shard_map/all_to_all | solution.py:15
where the time goes:
time: 109 us; the launch traced here: 108 us
  starting transfers between devices  43.7 us (40%)
  blocking collectives  38.4 us (35%)
  waiting for transfers between devices  11 us (10%)
  matrix products  6.26 us (6%)
  local copies, waits for them, and re-layouts  5.45 us (5%)
  other arithmetic  3.52 us (3%)
    all_to_all x1, starting transfers between devices, from_everyone(): return lax.all_to_all(copies, axis, split_axis=0, concat_axis=0, tiled=True)  43.7 us
    all_to_all x1, blocking collectives, summed_on_arrival(): lax.all_to_all(cut_along(shard, dim, devices), axis, 0, 0, tiled=True)  20 us
    all_to_all x1, blocking collectives, from_everyone(): return lax.all_to_all(copies, axis, split_axis=0, concat_axis=0, tiled=True)  18.4 us
    all_to_all x1, waiting for transfers between devices, from_everyone(): return lax.all_to_all(copies, axis, split_axis=0, concat_axis=0, tiled=True)  11 us
    dot_general x1, matrix products, project(): jnp.einsum('rthd,hdv->rthv', partial_value, weight.astype(jnp.float32), p...  2.2 us
  transfers between devices with their start and end apart: 1, of which 1 were waited for; matrix products, arithmetic and copies ran while one was open for 1% of the time, Pallas kernels for 0%

commit v1 on v0

v1 whole, which is shorter than its diff:
```python
import functools

import jax
import jax.numpy as jnp
from jax import lax
from jax.experimental import pallas as pl
from jax.experimental.pallas import tpu as pltpu
from jax.sharding import PartitionSpec as P


NOPE = 128
NEGATIVE = -1e30
STEPS = 32768.0
LEAST_EXPONENT = -110.0
WEIGHT_CHUNKS = 4


def decoded(message):
    half = message.shape[0] - 8
    log_weight = message[half : half + 1].astype(jnp.float32) * (1.0 / STEPS)
    exponent = message[half + 1 : half + 2].astype(jnp.float32)
    kept = message[half + 2 : half + 3] > 0
    packed = message[:half]
    high = jnp.right_shift(packed, 16).astype(jnp.float32)
    low = (jnp.bitwise_and(packed, 0xFFFF) - 32768).astype(jnp.float32)
    unit = jnp.exp2(exponent) * (1.0 / STEPS)
    return high, low, unit, log_weight, kept


def encoded(high, low, log_weight, kept):
    top = jnp.maximum(
        jnp.max(jnp.abs(high), axis=0, keepdims=True), jnp.max(jnp.abs(low), axis=0, keepdims=True)
    )
    exponent = jnp.maximum(jnp.ceil(jnp.log2(top)), LEAST_EXPONENT)
    factor = jnp.exp2(-exponent) * STEPS

    def fixed(x):
        return jnp.clip(jnp.round(x * factor), -32767.0, 32767.0).astype(jnp.int32)

    packed = fixed(high) * 65536 + (fixed(low) + 32768)
    rows = packed.shape[1]
    at = lax.broadcasted_iota(jnp.int32, (8, rows), 0)
    log_fixed = jnp.where(kept, jnp.round(log_weight * STEPS), 0.0).astype(jnp.int32)
    side = jnp.where(at == 0, log_fixed, 0)
    side = jnp.where(at == 1, exponent.astype(jnp.int32), side)
    side = jnp.where(at == 2, kept.astype(jnp.int32), side)
    return packed, side


def merged(messages):
    parts = [decoded(m) for m in messages]
    largest = functools.reduce(jnp.maximum, [jnp.where(p[4], p[3], NEGATIVE) for p in parts])
    weights = [jnp.where(p[4], jnp.exp(p[3] - largest), 0.0) for p in parts]
    total = sum(weights)
    kept = total > 0.0
    inverse = 1.0 / jnp.where(kept, total, 1.0)
    scales = [w * inverse * p[2] for w, p in zip(weights, parts)]
    high = sum(s * p[0] for s, p in zip(scales, parts))
    low = sum(s * p[1] for s, p in zip(scales, parts))
    return high, low, largest + jnp.log(jnp.where(kept, total, 1.0)), kept


def partial_kernel(
    lengths, slots, q_lat_hbm, q_rot_hbm, cache_hbm, rope_hbm, up_hbm, out_ref,
    q_lat, q_rot, cache, rope, up, attended, values, side, sems, cache_sems, rope_sems, up_sems,
):
    n_slots, page_len, latent = cache.shape
    _, tokens, heads, _ = q_lat.shape
    rows = tokens * heads
    step = heads // WEIGHT_CHUNKS
    copy = pltpu.make_async_copy
    q_copies = [copy(q_lat_hbm, q_lat, sems.at[0]), copy(q_rot_hbm, q_rot, sems.at[1])]
    cache_copies = [copy(cache_hbm.at[b], cache.at[b], cache_sems.at[b]) for b in range(n_slots)]
    rope_copies = [copy(rope_hbm.at[b], rope.at[b], rope_sems.at[b]) for b in range(n_slots)]
    up_copies = [
        copy(up_hbm.at[pl.ds(i * step, step)], up.at[pl.ds(i * step, step)], up_sems.at[i])
        for i in range(WEIGHT_CHUNKS)
    ]
    for c in q_copies:
        c.start()
    for pair in zip(cache_copies, rope_copies):
        for c in pair:
            c.start()
    for c in up_copies:
        c.start()
    softmax_scale = (NOPE + q_rot.shape[3]) ** -0.5
    first = lax.axis_index("seq") * page_len
    position = first + lax.broadcasted_iota(jnp.int32, (rows, page_len), 1)
    token = (lax.broadcasted_iota(jnp.int32, (rows, page_len), 0) >= heads).astype(jnp.int32)
    lane = lax.broadcasted_iota(jnp.int32, (rows, 128), 1)
    for c in q_copies:
        c.wait()
    for b in range(n_slots):
        request = slots[b]
        cache_copies[b].wait()
        rope_copies[b].wait()
        q1 = q_lat[request].reshape(rows, latent)
        q2 = q_rot[request].reshape(rows, -1)
        keys = cache[b]
        scores = lax.dot_general(
            q1, keys, (((1,), (1,)), ((), ())), preferred_element_type=jnp.float32
        )
        scores += jnp.dot(q2, rope[b], preferred_element_type=jnp.float32)
        visible = position < lengths[b] - (tokens - 1) + token
        masked = jnp.where(visible, scores * softmax_scale, NEGATIVE)
        page_max = jnp.max(masked, axis=1, keepdims=True)
        page_exp = jnp.where(visible, jnp.exp(masked - page_max), 0.0)
        page_den = jnp.sum(page_exp, axis=1, keepdims=True)
        kept = page_den > 0.0
        safe = jnp.where(kept, page_den, 1.0)
        page_out = jnp.dot(
            page_exp.astype(jnp.bfloat16), keys, preferred_element_type=jnp.float32
        )
        page_out *= 1.0 / safe
        for j in range(latent // 128):
            attended[j, pl.ds(b * rows, rows), :] = page_out[:, j * 128 : (j + 1) * 128]
        log_weight = page_max + jnp.log(safe)
        side[pl.ds(b * rows, rows), :] = jnp.where(
            lane == 0, log_weight, jnp.where(lane == 1, kept.astype(jnp.float32), 0.0)
        )
    pairs = n_slots * tokens
    for h in range(heads):
        if h % step == 0:
            up_copies[h // step].wait()
        x = jnp.concatenate(
            [attended[j, pl.ds(h, pairs, stride=heads), :] for j in range(latent // 128)], axis=1
        )
        high = x.astype(jnp.bfloat16)
        low = (x - high.astype(jnp.float32)).astype(jnp.bfloat16)
        y = jnp.dot(
            jnp.concatenate([high, low], axis=0), up[h], preferred_element_type=jnp.float32
        )
        values[pl.ds(h, pairs, stride=heads), :] = y[:pairs] + y[pairs:]
    columns = values[...].T
    sides = side[...].T
    half = columns.shape[0] // 2
    packed, words = encoded(columns[:half], columns[half:], sides[0:1], sides[1:2] > 0.5)
    out_ref[pl.ds(0, half), :] = packed
    out_ref[pl.ds(half, 8), :] = words


def local_message(q_latent, q_rope, cache_latent, rope_keys, lengths, slot_request, value_up):
    n_slots, _, latent = cache_latent.shape
    _, tokens, heads, _ = q_rope.shape
    dv = value_up.shape[2]
    rows = n_slots * tokens * heads
    hbm = pl.BlockSpec(memory_space=pl.ANY)
    smem = pl.BlockSpec(memory_space=pltpu.SMEM)
    return pl.pallas_call(
        partial_kernel,
        name="local_message",
        out_shape=pltpu.VMEM((dv // 2 + 8, rows), jnp.int32),
        in_specs=[smem, smem, hbm, hbm, hbm, hbm, hbm],
        out_specs=pl.BlockSpec(memory_space=pltpu.VMEM),
        scratch_shapes=[
            pltpu.VMEM(q_latent.shape, q_latent.dtype),
            pltpu.VMEM(q_rope.shape, q_rope.dtype),
            pltpu.VMEM(cache_latent.shape, cache_latent.dtype),
            pltpu.VMEM(rope_keys.shape, rope_keys.dtype),
            pltpu.VMEM(value_up.shape, value_up.dtype),
            pltpu.VMEM((latent // 128, rows, 128), jnp.float32),
            pltpu.VMEM((rows, dv), jnp.float32),
            pltpu.VMEM((rows, 128), jnp.float32),
            pltpu.SemaphoreType.DMA((2,)),
            pltpu.SemaphoreType.DMA((n_slots,)),
            pltpu.SemaphoreType.DMA((n_slots,)),
            pltpu.SemaphoreType.DMA((WEIGHT_CHUNKS,)),
        ],
    )(lengths, slot_request, q_latent, q_rope, cache_latent, rope_keys, value_up)


def merge_kernel(*refs):
    *ins, out_ref = refs
    half = out_ref.shape[0] - 8
    packed, words = encoded(*merged([r[...] for r in ins]))
    out_ref[pl.ds(0, half), :] = packed
    out_ref[pl.ds(half, 8), :] = words


def merge(*messages):
    vmem = pl.BlockSpec(memory_space=pltpu.VMEM)
    return pl.pallas_call(
        merge_kernel,
        name="merge",
        out_shape=pltpu.VMEM(messages[0].shape, jnp.int32),
        in_specs=[vmem] * len(messages),
        out_specs=vmem,
    )(*[pltpu.with_memory_space_constraint(m, pltpu.VMEM) for m in messages])


def finish_kernel(root, *refs):
    *ins, out_ref = refs
    high, low, _, _ = merged([r[...] for r in ins])
    whole = jnp.concatenate([high, low], axis=0)
    mine = lax.axis_index("seq") == root
    out_ref[...] = jnp.where(mine, whole.T, 0.0).astype(out_ref.dtype)


def finish(root, messages):
    half, rows = messages[0].shape
    vmem = pl.BlockSpec(memory_space=pltpu.VMEM)
    return pl.pallas_call(
        functools.partial(finish_kernel, root),
        name="finish",
        out_shape=pltpu.VMEM((rows, 2 * (half - 8)), jnp.bfloat16),
        in_specs=[vmem] * len(messages),
        out_specs=vmem,
    )(*[pltpu.with_memory_space_constraint(m, pltpu.VMEM) for m in messages])


def send(x, *pairs):
    return lax.ppermute(x, "seq", pairs)


ROOT = 1
LATE = (15, 10, 11, 12, 13, 14, 0, 9, 8)
EARLY = (7, 6, 5, 4, 3, 2)
RELAY = 15
TOLD = (0, 2, RELAY)
RELAYED = (3, 4, 5, 6, 7)
SPREAD = (((7, 8), (6, 9), (5, 10), (15, 14)), ((7, 11), (6, 12), (15, 13)))


def per_device(q_latent, q_rope, cache_latent, rope_keys, lengths, slot_request, value_up):
    own = local_message(q_latent, q_rope, cache_latent, rope_keys, lengths, slot_request, value_up)
    arrived = {z: send(own, (z, ROOT)) for z in LATE + EARLY}
    near = merge(own, *[arrived[z] for z in EARLY])
    held = finish(ROOT, [near, *[arrived[z] for z in LATE]])
    told = {z: send(held, (ROOT, z)) for z in TOLD}
    held = held + told.pop(RELAY)
    relayed = [send(held, (RELAY, z)) for z in RELAYED]
    held = sum(relayed, held)
    spread = [send(held, *pairs) for pairs in SPREAD]
    held = sum([*spread, *told.values()], held)
    n_slots, (_, tokens, heads, _) = cache_latent.shape[0], q_rope.shape
    return held.reshape(n_slots, tokens, heads, -1)


def solution(mesh):
    in_specs = (
        P("groups", None, "head", None),
        P("groups", None, "head", None),
        P(("groups", "rep"), "seq", None),
        P(("groups", "rep"), None, "seq"),
        P(("groups", "rep")),
        P(("groups", "rep")),
        P("head", None, None),
    )
    out_specs = P(("groups", "rep"), None, "head", None)
    return jax.shard_map(
        per_device, mesh=mesh, in_specs=in_specs, out_specs=out_specs, check_vma=False
    )
```

time: 109 us -> 85.5 us (0.78)
  blocking collectives: 38.4 us -> 0 us
  waiting for transfers between devices: 11 us -> 28 us
  Pallas kernels: 0 us -> 7.42 us
  matrix products: 6.26 us -> 0 us
  local copies, waits for them, and re-layouts: 5.45 us -> 0 us
  starting transfers between devices: 43.7 us -> 47.7 us
  other arithmetic: 3.52 us -> 0.7 us
    ppermute x0 -> x25, starting transfers between devices: none -> 47.7 us  [send(): return lax.ppermute(x, 'seq', pairs)]
    all_to_all x1 -> x0, starting transfers between devices: 43.7 us -> none  [from_everyone(): return lax.all_to_all(copies, axis, split_axis=0, concat_axis=0, tiled=True)]
    all_to_all x2 -> x0, blocking collectives: 38.4 us -> none  [the longest x1 20 us: summed_on_arrival(): lax.all_to_all(cut_along(shard, dim, devices), axis, 0, 0, tiled=True)]
    ppermute x0 -> x25, waiting for transfers between devices: none -> 28 us  [send(): return lax.ppermute(x, 'seq', pairs)]
    all_to_all x1 -> x0, waiting for transfers between devices: 11 us -> none  [from_everyone(): return lax.all_to_all(copies, axis, split_axis=0, concat_axis=0, tiled=True)]
    pallas_call x0 -> x3, Pallas kernels: none -> 7.42 us  [the longest x1 6.89 us: local_message(): pl.pallas_call(partial_kernel, name='local_message', out_shape=pltpu.VMEM...]
    dot_general x4 -> x0, matrix products: 6.26 us -> none  [the longest x1 2.2 us: project(): jnp.einsum('rthd,hdv->rthv', partial_value, weight.astype(jnp.float32), p...]
    gather x2 -> x0, local copies, waits for them, and re-layouts: 3.08 us -> none  [the longest x1 1.61 us: per_device(): query_lat = jnp.take(q_latent, slot_request, axis=0)]
  transfers between devices with their start and end apart: 1 -> 25, of which waited for: 1 -> 1; matrix products, arithmetic and copies ran while one was open for 1% -> 0% of each run, Pallas kernels for 0% -> 0%
where the time goes in v1:
time: 85.5 us; the launch traced here: 84.2 us
  starting transfers between devices  47.7 us (56%)
  waiting for transfers between devices  28 us (33%)
  Pallas kernels  7.42 us (9%)
    ppermute x25, starting transfers between devices, send(): return lax.ppermute(x, 'seq', pairs)  47.7 us
    ppermute x25, waiting for transfers between devices, send(): return lax.ppermute(x, 'seq', pairs)  28 us
    pallas_call x1, Pallas kernels, local_message(): pl.pallas_call(partial_kernel, name='local_message', out_shape=pltpu.VMEM...  6.89 us
  transfers between devices with their start and end apart: 25, of which 1 were waited for; matrix products, arithmetic and copies ran while one was open for 0% of the time, Pallas kernels for 0%

profile of v1, /device:TPU:80, one launch (start us, length us, event | category | flops | bytes accessed | tf_op | source)
XLA Modules:
  0.0 84.2 jit_solution(10805630991732176596)
XLA Ops:
  0.0 6.9 %local_message.1.refs_0_ = s32[72,256]{1,0:T(8,128)S(1)} custom-call(s32[8]{0:T(128)} %lengths.1, s32[8]{0:T(128)} %slots.1, bf16[16,2,16,512]{3,2,1,0:T(8,128)(2,1)} %q_lat_hbm.1, bf16[16,2,16,64]{3,2,1,0:T(8,128)(2,1)} %q_rot_hbm.1, bf16[8,128,512]{2,1,0:T(8,128)(2,1)} %cache_hbm.1, bf16[8,64,128]{2,1,0:T(8,128)(2,1)} %rope_hbm.1, bf16[16,512,128]{2,1,0:T(8,128)(2,1)} %up_hbm.1), custom_call_target="tpu_custom_call" | custom-call | tf_op jit(solution)/shard_map/local_message/pallas_call | solution.py:149
  6.9 0.7 collective-permute-start
  7.6 0.7 collective-permute-start.1
  8.2 0.7 collective-permute-start.2
  8.9 0.7 collective-permute-start.3
  9.6 0.7 collective-permute-start.4
  10.3 0.0 collective-permute-done.refs_1_
  10.3 0.7 collective-permute-start.5
  10.9 0.0 collective-permute-done.1.refs_2_
  11.0 0.7 collective-permute-start.10
  11.6 0.0 collective-permute-done.2.refs_3_
  11.6 0.7 collective-permute-start.11
  12.3 0.0 collective-permute-done.3.refs_4_
  12.3 31.1 %collective-permute-start.12 = (s32[72,256]{1,0:T(8,128)S(1)}, s32[72,256]{1,0:T(8,128)S(1)}, u32[]{:S(2)}, u32[]{:S(2)}) collective-permute-start(s32[72,256]{1,0:T(8,128)S(1)} %local_message.1.refs_0_), channel_id=1, source_target_pairs={{0,16},{1,17},{2,18},{3,19},{4,20},{5,21},{6,22},{7,23},{8,24},{9,... | collective-permute-start | bytes 221192 | tf_op jit(solution)/shard_map/ppermute | solution.py:212
  43.5 0.0 collective-permute-done.4.refs_5_
  43.5 0.7 collective-permute-start.13
  44.1 0.0 collective-permute-done.5.refs_6_
  44.1 0.7 collective-permute-start.14
  44.8 0.0 collective-permute-done.10.refs_5_
  44.8 0.7 collective-permute-start.6
  45.5 0.0 collective-permute-done.11.refs_6_
  45.5 0.7 collective-permute-start.7
  46.2 0.0 collective-permute-done.12.refs_7_
  46.2 0.7 collective-permute-start.8
  46.9 0.0 collective-permute-done.13.refs_8_
  46.9 0.7 collective-permute-start.9
  47.6 0.2 merge.1.refs_0_
  47.8 0.0 collective-permute-done.14.refs_9_
  47.8 0.0 collective-permute-done.6.refs_1_
  47.8 0.0 collective-permute-done.7.refs_2_
  47.8 0.0 collective-permute-done.8.refs_3_
  47.8 0.0 collective-permute-done.9.refs_4_
  47.8 0.3 finish.1
  48.2 0.7 collective-permute-start.15
  48.8 0.0 collective-permute-done.15
  48.9 0.7 collective-permute-start.16
  49.5 0.7 collective-permute-start.17
  50.2 0.7 collective-permute-start.18
  50.9 0.7 collective-permute-start.19
  51.6 0.7 collective-permute-start.20
  52.2 0.0 collective-permute-done.16
  52.2 1.3 %collective-permute-start.23 = (bf16[256,128]{1,0:T(8,128)(2,1)S(1)}, bf16[256,128]{1,0:T(8,128)(2,1)S(1)}, u32[]{:S(2)}, u32[]{:S(2)}) collective-permute-start(bf16[256,128]{1,0:T(8,128)(2,1)S(1)} %finish.1), channel_id=1, source_target_pairs={{16,0},{17,1},{18,2},{19,3},{20,4},{21,5},{22,6},{23,7},{24,8},{25... | collective-permute-start | bytes 196616 | tf_op jit(solution)/shard_map/ppermute | solution.py:212
  53.6 0.0 collective-permute-done.17
  53.6 0.7 collective-permute-start.24
  54.2 0.0 collective-permute-done.18
  54.3 0.0 collective-permute-done.19
  54.3 0.0 collective-permute-done.20
  54.3 0.7 collective-permute-start.21
  55.0 0.7 collective-permute-start.22
  55.7 27.9 %collective-permute-done.23 = bf16[256,128]{1,0:T(8,128)(2,1)S(1)} collective-permute-done((bf16[256,128]{1,0:T(8,128)(2,1)S(1)}, bf16[256,128]{1,0:T(8,128)(2,1)S(1)}, u32[]{:S(2)}, u32[]{:S(2)}) %collective-permute-start.23) | collective-permute-done | bytes 65568 | tf_op jit(solution)/shard_map/ppermute | solution.py:212
  83.6 0.0 collective-permute-done.24
  83.6 0.0 collective-permute-done.21
  83.6 0.0 collective-permute-done.22
  83.6 0.7 add_add_fusion
  (2 shorter events, 0.0 us)
Async XLA Ops:
  6.9 3.4 %collective-permute-start = (s32[72,256]{1,0:T(8,128)S(1)}, s32[72,256]{1,0:T(8,128)S(1)}, u32[]{:S(2)}, u32[]{:S(2)}) collective-permute-start(s32[72,256]{1,0:T(8,128)S(1)} %local_message.1.refs_0_), channel_id=1, source_target_pairs={{112,16},{113,17},{114,18},{115,19},{116,20},{117,21},{118,22},{11... | collective-permute-start | bytes 221192 | tf_op jit(solution)/shard_map/ppermute | solution.py:212
  7.6 3.4 %collective-permute-start.1 = (s32[72,256]{1,0:T(8,128)S(1)}, s32[72,256]{1,0:T(8,128)S(1)}, u32[]{:S(2)}, u32[]{:S(2)}) collective-permute-start(s32[72,256]{1,0:T(8,128)S(1)} %local_message.1.refs_0_), channel_id=1, source_target_pairs={{96,16},{97,17},{98,18},{99,19},{100,20},{101,21},{102,22},{103,23... | collective-permute-start | bytes 221192 | tf_op jit(solution)/shard_map/ppermute | solution.py:212
  8.2 3.4 %collective-permute-start.2 = (s32[72,256]{1,0:T(8,128)S(1)}, s32[72,256]{1,0:T(8,128)S(1)}, u32[]{:S(2)}, u32[]{:S(2)}) collective-permute-start(s32[72,256]{1,0:T(8,128)S(1)} %local_message.1.refs_0_), channel_id=1, source_target_pairs={{80,16},{81,17},{82,18},{83,19},{84,20},{85,21},{86,22},{87,23},{8... | collective-permute-start | bytes 221192 | tf_op jit(solution)/shard_map/ppermute | solution.py:212
  8.9 3.4 %collective-permute-start.3 = (s32[72,256]{1,0:T(8,128)S(1)}, s32[72,256]{1,0:T(8,128)S(1)}, u32[]{:S(2)}, u32[]{:S(2)}) collective-permute-start(s32[72,256]{1,0:T(8,128)S(1)} %local_message.1.refs_0_), channel_id=1, source_target_pairs={{64,16},{65,17},{66,18},{67,19},{68,20},{69,21},{70,22},{71,23},{7... | collective-permute-start | bytes 221192 | tf_op jit(solution)/shard_map/ppermute | solution.py:212
  9.6 33.9 %collective-permute-start.4 = (s32[72,256]{1,0:T(8,128)S(1)}, s32[72,256]{1,0:T(8,128)S(1)}, u32[]{:S(2)}, u32[]{:S(2)}) collective-permute-start(s32[72,256]{1,0:T(8,128)S(1)} %local_message.1.refs_0_), channel_id=1, source_target_pairs={{48,16},{49,17},{50,18},{51,19},{52,20},{53,21},{54,22},{55,23},{5... | collective-permute-start | bytes 221192 | tf_op jit(solution)/shard_map/ppermute | solution.py:212
  10.3 33.9 %collective-permute-start.5 = (s32[72,256]{1,0:T(8,128)S(1)}, s32[72,256]{1,0:T(8,128)S(1)}, u32[]{:S(2)}, u32[]{:S(2)}) collective-permute-start(s32[72,256]{1,0:T(8,128)S(1)} %local_message.1.refs_0_), channel_id=1, source_target_pairs={{32,16},{33,17},{34,18},{35,19},{36,20},{37,21},{38,22},{39,23},{4... | collective-permute-start | bytes 221192 | tf_op jit(solution)/shard_map/ppermute | solution.py:212
  11.0 33.9 %collective-permute-start.10 = (s32[72,256]{1,0:T(8,128)S(1)}, s32[72,256]{1,0:T(8,128)S(1)}, u32[]{:S(2)}, u32[]{:S(2)}) collective-permute-start(s32[72,256]{1,0:T(8,128)S(1)} %local_message.1.refs_0_), channel_id=1, source_target_pairs={{208,16},{209,17},{210,18},{211,19},{212,20},{213,21},{214,22},{21... | collective-permute-start | bytes 221192 | tf_op jit(solution)/shard_map/ppermute | solution.py:212
  11.6 33.9 %collective-permute-start.11 = (s32[72,256]{1,0:T(8,128)S(1)}, s32[72,256]{1,0:T(8,128)S(1)}, u32[]{:S(2)}, u32[]{:S(2)}) collective-permute-start(s32[72,256]{1,0:T(8,128)S(1)} %local_message.1.refs_0_), channel_id=1, source_target_pairs={{224,16},{225,17},{226,18},{227,19},{228,20},{229,21},{230,22},{23... | collective-permute-start | bytes 221192 | tf_op jit(solution)/shard_map/ppermute | solution.py:212
  12.3 33.9 %collective-permute-start.12 = (s32[72,256]{1,0:T(8,128)S(1)}, s32[72,256]{1,0:T(8,128)S(1)}, u32[]{:S(2)}, u32[]{:S(2)}) collective-permute-start(s32[72,256]{1,0:T(8,128)S(1)} %local_message.1.refs_0_), channel_id=1, source_target_pairs={{0,16},{1,17},{2,18},{3,19},{4,20},{5,21},{6,22},{7,23},{8,24},{9,... | collective-permute-start | bytes 221192 | tf_op jit(solution)/shard_map/ppermute | solution.py:212
  43.5 3.4 %collective-permute-start.13 = (s32[72,256]{1,0:T(8,128)S(1)}, s32[72,256]{1,0:T(8,128)S(1)}, u32[]{:S(2)}, u32[]{:S(2)}) collective-permute-start(s32[72,256]{1,0:T(8,128)S(1)} %local_message.1.refs_0_), channel_id=1, source_target_pairs={{144,16},{145,17},{146,18},{147,19},{148,20},{149,21},{150,22},{15... | collective-permute-start | bytes 221192 | tf_op jit(solution)/shard_map/ppermute | solution.py:212
  44.1 3.6 %collective-permute-start.14 = (s32[72,256]{1,0:T(8,128)S(1)}, s32[72,256]{1,0:T(8,128)S(1)}, u32[]{:S(2)}, u32[]{:S(2)}) collective-permute-start(s32[72,256]{1,0:T(8,128)S(1)} %local_message.1.refs_0_), channel_id=1, source_target_pairs={{128,16},{129,17},{130,18},{131,19},{132,20},{133,21},{134,22},{13... | collective-permute-start | bytes 221192 | tf_op jit(solution)/shard_map/ppermute | solution.py:212
  44.8 3.0 %collective-permute-start.6 = (s32[72,256]{1,0:T(8,128)S(1)}, s32[72,256]{1,0:T(8,128)S(1)}, u32[]{:S(2)}, u32[]{:S(2)}) collective-permute-start(s32[72,256]{1,0:T(8,128)S(1)} %local_message.1.refs_0_), channel_id=1, source_target_pairs={{240,16},{241,17},{242,18},{243,19},{244,20},{245,21},{246,22},{24... | collective-permute-start | bytes 221192 | tf_op jit(solution)/shard_map/ppermute | solution.py:212
  45.5 2.3 %collective-permute-start.7 = (s32[72,256]{1,0:T(8,128)S(1)}, s32[72,256]{1,0:T(8,128)S(1)}, u32[]{:S(2)}, u32[]{:S(2)}) collective-permute-start(s32[72,256]{1,0:T(8,128)S(1)} %local_message.1.refs_0_), channel_id=1, source_target_pairs={{160,16},{161,17},{162,18},{163,19},{164,20},{165,21},{166,22},{16... | collective-permute-start | bytes 221192 | tf_op jit(solution)/shard_map/ppermute | solution.py:212
  46.2 1.6 %collective-permute-start.8 = (s32[72,256]{1,0:T(8,128)S(1)}, s32[72,256]{1,0:T(8,128)S(1)}, u32[]{:S(2)}, u32[]{:S(2)}) collective-permute-start(s32[72,256]{1,0:T(8,128)S(1)} %local_message.1.refs_0_), channel_id=1, source_target_pairs={{176,16},{177,17},{178,18},{179,19},{180,20},{181,21},{182,22},{18... | collective-permute-start | bytes 221192 | tf_op jit(solution)/shard_map/ppermute | solution.py:212
  46.9 0.9 %collective-permute-start.9 = (s32[72,256]{1,0:T(8,128)S(1)}, s32[72,256]{1,0:T(8,128)S(1)}, u32[]{:S(2)}, u32[]{:S(2)}) collective-permute-start(s32[72,256]{1,0:T(8,128)S(1)} %local_message.1.refs_0_), channel_id=1, source_target_pairs={{192,16},{193,17},{194,18},{195,19},{196,20},{197,21},{198,22},{19... | collective-permute-start | bytes 221192 | tf_op jit(solution)/shard_map/ppermute | solution.py:212
  48.2 0.7 collective-permute-start.15
  48.9 3.4 %collective-permute-start.16 = (bf16[256,128]{1,0:T(8,128)(2,1)S(1)}, bf16[256,128]{1,0:T(8,128)(2,1)S(1)}, u32[]{:S(2)}, u32[]{:S(2)}) collective-permute-start(bf16[256,128]{1,0:T(8,128)(2,1)S(1)} %add.30), channel_id=1, source_target_pairs={{240,48},{241,49},{242,50},{243,51},{244,52},{245,53},{246,54},{24... | collective-permute-start | bytes 196616 | tf_op jit(solution)/shard_map/ppermute | solution.py:212
  49.5 4.0 %collective-permute-start.17 = (bf16[256,128]{1,0:T(8,128)(2,1)S(1)}, bf16[256,128]{1,0:T(8,128)(2,1)S(1)}, u32[]{:S(2)}, u32[]{:S(2)}) collective-permute-start(bf16[256,128]{1,0:T(8,128)(2,1)S(1)} %add.30), channel_id=1, source_target_pairs={{240,64},{241,65},{242,66},{243,67},{244,68},{245,69},{246,70},{24... | collective-permute-start | bytes 196616 | tf_op jit(solution)/shard_map/ppermute | solution.py:212
  50.2 4.0 %collective-permute-start.18 = (bf16[256,128]{1,0:T(8,128)(2,1)S(1)}, bf16[256,128]{1,0:T(8,128)(2,1)S(1)}, u32[]{:S(2)}, u32[]{:S(2)}) collective-permute-start(bf16[256,128]{1,0:T(8,128)(2,1)S(1)} %add.30), channel_id=1, source_target_pairs={{240,80},{241,81},{242,82},{243,83},{244,84},{245,85},{246,86},{24... | collective-permute-start | bytes 196616 | tf_op jit(solution)/shard_map/ppermute | solution.py:212
  50.9 3.4 %collective-permute-start.19 = (bf16[256,128]{1,0:T(8,128)(2,1)S(1)}, bf16[256,128]{1,0:T(8,128)(2,1)S(1)}, u32[]{:S(2)}, u32[]{:S(2)}) collective-permute-start(bf16[256,128]{1,0:T(8,128)(2,1)S(1)} %add.30), channel_id=1, source_target_pairs={{240,96},{241,97},{242,98},{243,99},{244,100},{245,101},{246,102},... | collective-permute-start | bytes 196616 | tf_op jit(solution)/shard_map/ppermute | solution.py:212
  51.6 2.7 %collective-permute-start.20 = (bf16[256,128]{1,0:T(8,128)(2,1)S(1)}, bf16[256,128]{1,0:T(8,128)(2,1)S(1)}, u32[]{:S(2)}, u32[]{:S(2)}) collective-permute-start(bf16[256,128]{1,0:T(8,128)(2,1)S(1)} %add.30), channel_id=1, source_target_pairs={{240,112},{241,113},{242,114},{243,115},{244,116},{245,117},{246,1... | collective-permute-start | bytes 196616 | tf_op jit(solution)/shard_map/ppermute | solution.py:212
  52.2 31.3 %collective-permute-start.23 = (bf16[256,128]{1,0:T(8,128)(2,1)S(1)}, bf16[256,128]{1,0:T(8,128)(2,1)S(1)}, u32[]{:S(2)}, u32[]{:S(2)}) collective-permute-start(bf16[256,128]{1,0:T(8,128)(2,1)S(1)} %finish.1), channel_id=1, source_target_pairs={{16,0},{17,1},{18,2},{19,3},{20,4},{21,5},{22,6},{23,7},{24,8},{25... | collective-permute-start | bytes 196616 | tf_op jit(solution)/shard_map/ppermute | solution.py:212
  53.6 30.0 %collective-permute-start.24 = (bf16[256,128]{1,0:T(8,128)(2,1)S(1)}, bf16[256,128]{1,0:T(8,128)(2,1)S(1)}, u32[]{:S(2)}, u32[]{:S(2)}) collective-permute-start(bf16[256,128]{1,0:T(8,128)(2,1)S(1)} %finish.1), channel_id=1, source_target_pairs={{16,32},{17,33},{18,34},{19,35},{20,36},{21,37},{22,38},{23,39},{2... | collective-permute-start | bytes 196616 | tf_op jit(solution)/shard_map/ppermute | solution.py:212
  54.3 29.3 %collective-permute-start.21 = (bf16[256,128]{1,0:T(8,128)(2,1)S(1)}, bf16[256,128]{1,0:T(8,128)(2,1)S(1)}, u32[]{:S(2)}, u32[]{:S(2)}) collective-permute-start(bf16[256,128]{1,0:T(8,128)(2,1)S(1)} %add_add_fusion.1), channel_id=1, source_target_pairs={{112,128},{96,144},{80,160},{240,224},{113,129},{97,145},{81,161},... | collective-permute-start | bytes 196616 | tf_op jit(solution)/shard_map/ppermute | solution.py:212
  55.0 28.6 %collective-permute-start.22 = (bf16[256,128]{1,0:T(8,128)(2,1)S(1)}, bf16[256,128]{1,0:T(8,128)(2,1)S(1)}, u32[]{:S(2)}, u32[]{:S(2)}) collective-permute-start(bf16[256,128]{1,0:T(8,128)(2,1)S(1)} %add_add_fusion.1), channel_id=1, source_target_pairs={{112,176},{96,192},{240,208},{113,177},{97,193},{241,209},{114,178... | collective-permute-start | bytes 196616 | tf_op jit(solution)/shard_map/ppermute | solution.py:212

commit v2 on v1

--- a/solution.py
+++ b/solution.py
@@ -12,7 +12,8 @@
 NEGATIVE = -1e30
 STEPS = 32768.0
 LEAST_EXPONENT = -110.0
-WEIGHT_CHUNKS = 4
+WEIGHT_CHUNKS = 1
+PAGE_GROUPS = 1
 
 
 def decoded(message):
@@ -61,67 +62,78 @@
 
 
 def partial_kernel(
-    lengths, slots, q_lat_hbm, q_rot_hbm, cache_hbm, rope_hbm, up_hbm, out_ref,
-    q_lat, q_rot, cache, rope, up, attended, values, side, sems, cache_sems, rope_sems, up_sems,
+    lengths_hbm, slots_hbm, q_lat_hbm, q_rot_hbm, cache_hbm, rope_hbm, up_hbm, out_ref,
+    lengths, slots, q_lat, q_rot, cache, rope, up, attended, values, side, sems, page_sems, up_sems,
 ):
     n_slots, page_len, latent = cache.shape
     _, tokens, heads, _ = q_lat.shape
     rows = tokens * heads
     step = heads // WEIGHT_CHUNKS
+    group = n_slots // PAGE_GROUPS
     copy = pltpu.make_async_copy
-    q_copies = [copy(q_lat_hbm, q_lat, sems.at[0]), copy(q_rot_hbm, q_rot, sems.at[1])]
-    cache_copies = [copy(cache_hbm.at[b], cache.at[b], cache_sems.at[b]) for b in range(n_slots)]
-    rope_copies = [copy(rope_hbm.at[b], rope.at[b], rope_sems.at[b]) for b in range(n_slots)]
-    up_copies = [
+    scalars = [copy(lengths_hbm, lengths, sems.at[0]), copy(slots_hbm, slots, sems.at[1])]
+    queries = [copy(q_lat_hbm, q_lat, sems.at[2]), copy(q_rot_hbm, q_rot, sems.at[3])]
+    pages = []
+    for g in range(PAGE_GROUPS):
+        at = pl.ds(g * group, group)
+        pages.append(
+            [
+                copy(cache_hbm.at[at], cache.at[at], page_sems.at[g, 0]),
+                copy(rope_hbm.at[at], rope.at[at], page_sems.at[g, 1]),
+            ]
+        )
+    ups = [
         copy(up_hbm.at[pl.ds(i * step, step)], up.at[pl.ds(i * step, step)], up_sems.at[i])
         for i in range(WEIGHT_CHUNKS)
     ]
-    for c in q_copies:
-        c.start()
-    for pair in zip(cache_copies, rope_copies):
-        for c in pair:
-            c.start()
-    for c in up_copies:
+    for c in [*scalars, *queries, *sum(pages, []), *ups]:
         c.start()
     softmax_scale = (NOPE + q_rot.shape[3]) ** -0.5
     first = lax.axis_index("seq") * page_len
-    position = first + lax.broadcasted_iota(jnp.int32, (rows, page_len), 1)
     token = (lax.broadcasted_iota(jnp.int32, (rows, page_len), 0) >= heads).astype(jnp.int32)
+    offset = first + lax.broadcasted_iota(jnp.int32, (rows, page_len), 1) - token + (tokens - 1)
     lane = lax.broadcasted_iota(jnp.int32, (rows, 128), 1)
-    for c in q_copies:
+    for c in [*scalars, *queries]:
         c.wait()
-    for b in range(n_slots):
-        request = slots[b]
-        cache_copies[b].wait()
-        rope_copies[b].wait()
-        q1 = q_lat[request].reshape(rows, latent)
-        q2 = q_rot[request].reshape(rows, -1)
-        keys = cache[b]
-        scores = lax.dot_general(
-            q1, keys, (((1,), (1,)), ((), ())), preferred_element_type=jnp.float32
-        )
-        scores += jnp.dot(q2, rope[b], preferred_element_type=jnp.float32)
-        visible = position < lengths[b] - (tokens - 1) + token
-        masked = jnp.where(visible, scores * softmax_scale, NEGATIVE)
-        page_max = jnp.max(masked, axis=1, keepdims=True)
-        page_exp = jnp.where(visible, jnp.exp(masked - page_max), 0.0)
-        page_den = jnp.sum(page_exp, axis=1, keepdims=True)
-        kept = page_den > 0.0
-        safe = jnp.where(kept, page_den, 1.0)
-        page_out = jnp.dot(
-            page_exp.astype(jnp.bfloat16), keys, preferred_element_type=jnp.float32
-        )
-        page_out *= 1.0 / safe
-        for j in range(latent // 128):
-            attended[j, pl.ds(b * rows, rows), :] = page_out[:, j * 128 : (j + 1) * 128]
-        log_weight = page_max + jnp.log(safe)
-        side[pl.ds(b * rows, rows), :] = jnp.where(
-            lane == 0, log_weight, jnp.where(lane == 1, kept.astype(jnp.float32), 0.0)
-        )
+    for g in range(PAGE_GROUPS):
+        for c in pages[g]:
+            c.wait()
+        members = range(g * group, (g + 1) * group)
+        scores = []
+        for b in members:
+            request = slots[b]
+            q1 = q_lat[request].reshape(rows, latent)
+            q2 = q_rot[request].reshape(rows, -1)
+            s = lax.dot_general(
+                q1, cache[b], (((1,), (1,)), ((), ())), preferred_element_type=jnp.float32
+            )
+            scores.append(s + jnp.dot(q2, rope[b], preferred_element_type=jnp.float32))
+        weights = []
+        for b, s in zip(members, scores):
+            visible = offset < lengths[b]
+            masked = jnp.where(visible, s * softmax_scale, NEGATIVE)
+            page_max = jnp.max(masked, axis=1, keepdims=True)
+            page_exp = jnp.where(visible, jnp.exp(masked - page_max), 0.0)
+            weights.append((page_max, page_exp))
+        for b, (page_max, page_exp) in zip(members, weights):
+            page_out = jnp.dot(
+                page_exp.astype(jnp.bfloat16), cache[b], preferred_element_type=jnp.float32
+            )
+            page_den = jnp.sum(page_exp, axis=1, keepdims=True)
+            kept = page_den > 0.0
+            safe = jnp.where(kept, page_den, 1.0)
+            page_out *= 1.0 / safe
+            for j in range(latent // 128):
+                attended[j, pl.ds(b * rows, rows), :] = page_out[:, j * 128 : (j + 1) * 128]
+            side[pl.ds(b * rows, rows), :] = jnp.where(
+                lane == 0,
+                page_max + jnp.log(safe),
+                jnp.where(lane == 1, kept.astype(jnp.float32), 0.0),
+            )
     pairs = n_slots * tokens
     for h in range(heads):
         if h % step == 0:
-            up_copies[h // step].wait()
+            ups[h // step].wait()
         x = jnp.concatenate(
             [attended[j, pl.ds(h, pairs, stride=heads), :] for j in range(latent // 128)], axis=1
         )
@@ -140,19 +152,20 @@
 
 
 def local_message(q_latent, q_rope, cache_latent, rope_keys, lengths, slot_request, value_up):
-    n_slots, _, latent = cache_latent.shape
+    n_slots = cache_latent.shape[0]
+    latent = cache_latent.shape[2]
     _, tokens, heads, _ = q_rope.shape
     dv = value_up.shape[2]
     rows = n_slots * tokens * heads
-    hbm = pl.BlockSpec(memory_space=pl.ANY)
-    smem = pl.BlockSpec(memory_space=pltpu.SMEM)
     return pl.pallas_call(
         partial_kernel,
         name="local_message",
         out_shape=pltpu.VMEM((dv // 2 + 8, rows), jnp.int32),
-        in_specs=[smem, smem, hbm, hbm, hbm, hbm, hbm],
+        in_specs=[pl.BlockSpec(memory_space=pl.ANY)] * 7,
         out_specs=pl.BlockSpec(memory_space=pltpu.VMEM),
         scratch_shapes=[
+            pltpu.SMEM(lengths.shape, jnp.int32),
+            pltpu.SMEM(slot_request.shape, jnp.int32),
             pltpu.VMEM(q_latent.shape, q_latent.dtype),
             pltpu.VMEM(q_rope.shape, q_rope.dtype),
             pltpu.VMEM(cache_latent.shape, cache_latent.dtype),
@@ -161,9 +174,8 @@
             pltpu.VMEM((latent // 128, rows, 128), jnp.float32),
             pltpu.VMEM((rows, dv), jnp.float32),
             pltpu.VMEM((rows, 128), jnp.float32),
-            pltpu.SemaphoreType.DMA((2,)),
-            pltpu.SemaphoreType.DMA((n_slots,)),
-            pltpu.SemaphoreType.DMA((n_slots,)),
+            pltpu.SemaphoreType.DMA((4,)),
+            pltpu.SemaphoreType.DMA((PAGE_GROUPS, 2)),
             pltpu.SemaphoreType.DMA((WEIGHT_CHUNKS,)),
         ],
     )(lengths, slot_request, q_latent, q_rope, cache_latent, rope_keys, value_up)
@@ -212,26 +224,35 @@
     return lax.ppermute(x, "seq", pairs)
 
 
-ROOT = 1
+ROOT = 2
 LATE = (15, 10, 11, 12, 13, 14, 0, 9, 8)
-EARLY = (7, 6, 5, 4, 3, 2)
-RELAY = 15
-TOLD = (0, 2, RELAY)
-RELAYED = (3, 4, 5, 6, 7)
-SPREAD = (((7, 8), (6, 9), (5, 10), (15, 14)), ((7, 11), (6, 12), (15, 13)))
+TREE = (((3, 2), (7, 6), (5, 4)), ((1, 2), (6, 4)), ((4, 2),))
+FAN = (
+    ('fan0', (), ((2, 0),)),
+    ('fan1', (), ((2, 5),)),
+    ('fan2', (), ((2, 1),)),
+    ('fan3', ('fan1',), ((5, 3),)),
+    ('fan4', ('fan1',), ((5, 4),)),
+    ('fan5', ('fan1',), ((5, 8),)),
+    ('fan6', ('fan1',), ((5, 12),)),
+    ('fan7', ('fan1', 'fan5', 'fan6'), ((5, 6), (8, 10), (12, 14))),
+    ('fan8', ('fan1', 'fan5', 'fan6', 'fan7'), ((5, 7), (8, 9), (10, 11), (12, 13), (14, 15))),
+)
 
 
 def per_device(q_latent, q_rope, cache_latent, rope_keys, lengths, slot_request, value_up):
     own = local_message(q_latent, q_rope, cache_latent, rope_keys, lengths, slot_request, value_up)
-    arrived = {z: send(own, (z, ROOT)) for z in LATE + EARLY}
-    near = merge(own, *[arrived[z] for z in EARLY])
-    held = finish(ROOT, [near, *[arrived[z] for z in LATE]])
-    told = {z: send(held, (ROOT, z)) for z in TOLD}
-    held = held + told.pop(RELAY)
-    relayed = [send(held, (RELAY, z)) for z in RELAYED]
-    held = sum(relayed, held)
-    spread = [send(held, *pairs) for pairs in SPREAD]
-    held = sum([*spread, *told.values()], held)
+    late = [send(own, (z, ROOT)) for z in LATE]
+    near = [own]
+    for i, pairs in enumerate(TREE):
+        if i:
+            near = [merge(*near)]
+        near.append(send(near[0], *pairs))
+    held = finish(ROOT, [*near, *late])
+    got = {}
+    for name, needs, pairs in FAN:
+        got[name] = send(sum([got[n] for n in needs], held), *pairs)
+    held = sum(got.values(), held)
     n_slots, (_, tokens, heads, _) = cache_latent.shape[0], q_rope.shape
     return held.reshape(n_slots, tokens, heads, -1)
 

time: 85.5 us -> 81.6 us (0.954)
  the two profiles are of different devices: /device:TPU:80 before, /device:TPU:448 now
where the time goes in v2:
time: 81.6 us; the launch traced here: 81.2 us
  waiting for transfers between devices  61.4 us (75%)
  starting transfers between devices  15.3 us (19%)
  Pallas kernels  3.47 us (4%)
    ppermute x21, waiting for transfers between devices, send(): return lax.ppermute(x, 'seq', pairs)  61.4 us
    ppermute x21, starting transfers between devices, send(): return lax.ppermute(x, 'seq', pairs)  15.3 us
    pallas_call x1, Pallas kernels, local_message(): pl.pallas_call(partial_kernel, name='local_message', out_shape=pltpu.VMEM...  2.93 us
  transfers between devices with their start and end apart: 21, of which 2 were waited for; matrix products, arithmetic and copies ran while one was open for 0% of the time, Pallas kernels for 0%

profile of v2, /device:TPU:448, one launch (start us, length us, event | category | flops | bytes accessed | tf_op | source)
XLA Modules:
  0.0 81.2 jit_solution(13395335779276311340)
XLA Ops:
  0.0 2.9 %local_message.1.refs_0_ = s32[72,256]{1,0:T(8,128)S(1)} custom-call(s32[8]{0:T(128)} %lengths_hbm.1, s32[8]{0:T(128)} %slots_hbm.1, bf16[16,2,16,512]{3,2,1,0:T(8,128)(2,1)} %q_lat_hbm.1, bf16[16,2,16,64]{3,2,1,0:T(8,128)(2,1)} %q_rot_hbm.1, bf16[8,128,512]{2,1,0:T(8,128)(2,1)} %cache_hbm.1, bf16[8,64,128]{2,1,0:T(8,128)(2,1)} %rope_hbm.1, ...), custom_call_target="tpu_custom_call" | custom-call | tf_op jit(solution)/shard_map/local_message/pallas_call | solution.py:160
  2.9 1.3 %collective-permute-start = (s32[72,256]{1,0:T(8,128)S(1)}, s32[72,256]{1,0:T(8,128)S(1)}, u32[]{:S(2)}, u32[]{:S(2)}) collective-permute-start(s32[72,256]{1,0:T(8,128)S(1)} %local_message.1.refs_0_), channel_id=1, source_target_pairs={{48,32},{112,96},{80,64},{49,33},{113,97},{81,65},{50,34},{114,98}... | collective-permute-start | bytes 221192 | tf_op jit(solution)/shard_map/ppermute | solution.py:224
  4.3 2.0 %collective-permute-done.refs_1_ = s32[72,256]{1,0:T(8,128)S(1)} collective-permute-done((s32[72,256]{1,0:T(8,128)S(1)}, s32[72,256]{1,0:T(8,128)S(1)}, u32[]{:S(2)}, u32[]{:S(2)}) %collective-permute-start) | collective-permute-done | bytes 73760 | tf_op jit(solution)/shard_map/ppermute | solution.py:224
  6.2 0.1 merge.2.refs_0_
  6.3 0.7 collective-permute-start.1
  7.0 0.7 collective-permute-start.11
  7.7 0.7 collective-permute-start.10
  8.3 0.7 collective-permute-start.9
  9.0 0.7 collective-permute-start.8
  9.7 0.0 collective-permute-done.1.refs_1_
  9.7 0.7 collective-permute-start.7
  10.4 0.1 merge.3.refs_0_
  10.5 0.0 collective-permute-done.11.refs_10_
  10.5 0.7 collective-permute-start.6
  11.2 0.0 collective-permute-done.10.refs_9_
  11.2 0.7 collective-permute-start.5
  11.8 0.0 collective-permute-done.9.refs_8_
  11.8 0.7 collective-permute-start.4
  12.5 0.0 collective-permute-done.8.refs_7_
  12.5 0.7 collective-permute-start.3
  13.2 0.0 collective-permute-done.7.refs_6_
  13.2 0.7 collective-permute-start.2
  13.9 0.0 collective-permute-done.6.refs_5_
  13.9 0.0 collective-permute-done.5.refs_4_
  13.9 0.0 collective-permute-done.4.refs_3_
  13.9 0.0 collective-permute-done.3.refs_2_
  13.9 0.0 collective-permute-done.2.refs_1_
  13.9 0.3 finish.1
  14.3 0.7 collective-permute-start.13
  15.0 0.0 collective-permute-done.13
  15.0 0.7 collective-permute-start.18
  15.7 0.7 collective-permute-start.17
  16.3 0.0 collective-permute-done.18
  16.4 0.0 collective-permute-done.17
  16.4 0.7 collective-permute-start.19
  17.1 0.7 collective-permute-start.14
  17.7 0.7 collective-permute-start.12
  18.4 0.7 collective-permute-start.16
  19.1 1.3 %collective-permute-start.15 = (bf16[256,128]{1,0:T(8,128)(2,1)S(1)}, bf16[256,128]{1,0:T(8,128)(2,1)S(1)}, u32[]{:S(2)}, u32[]{:S(2)}) collective-permute-start(bf16[256,128]{1,0:T(8,128)(2,1)S(1)} %add.49), channel_id=1, source_target_pairs={{80,48},{81,49},{82,50},{83,51},{84,52},{85,53},{86,54},{87,55},{8... | collective-permute-start | bytes 196616 | tf_op jit(solution)/shard_map/ppermute | solution.py:224
  20.4 0.0 collective-permute-done.19
  20.4 0.7 collective-permute-start.20
  21.1 0.0 collective-permute-done.14
  21.1 0.0 collective-permute-done.12
  21.1 0.0 collective-permute-done.16
  21.1 59.4 %collective-permute-done.15 = bf16[256,128]{1,0:T(8,128)(2,1)S(1)} collective-permute-done((bf16[256,128]{1,0:T(8,128)(2,1)S(1)}, bf16[256,128]{1,0:T(8,128)(2,1)S(1)}, u32[]{:S(2)}, u32[]{:S(2)}) %collective-permute-start.15) | collective-permute-done | bytes 65568 | tf_op jit(solution)/shard_map/ppermute | solution.py:224
  80.5 0.0 collective-permute-done.20
  80.5 0.7 add_add_fusion
  (3 shorter events, 0.1 us)
Async XLA Ops:
  2.9 3.3 %collective-permute-start = (s32[72,256]{1,0:T(8,128)S(1)}, s32[72,256]{1,0:T(8,128)S(1)}, u32[]{:S(2)}, u32[]{:S(2)}) collective-permute-start(s32[72,256]{1,0:T(8,128)S(1)} %local_message.1.refs_0_), channel_id=1, source_target_pairs={{48,32},{112,96},{80,64},{49,33},{113,97},{81,65},{50,34},{114,98}... | collective-permute-start | bytes 221192 | tf_op jit(solution)/shard_map/ppermute | solution.py:224
  6.3 3.4 %collective-permute-start.1 = (s32[72,256]{1,0:T(8,128)S(1)}, s32[72,256]{1,0:T(8,128)S(1)}, u32[]{:S(2)}, u32[]{:S(2)}) collective-permute-start(s32[72,256]{1,0:T(8,128)S(1)} %merge.2.refs_0_), channel_id=1, source_target_pairs={{16,32},{96,64},{17,33},{97,65},{18,34},{98,66},{19,35},{99,67},{2... | collective-permute-start | bytes 221192 | tf_op jit(solution)/shard_map/ppermute | solution.py:224
  7.0 3.5 %collective-permute-start.11 = (s32[72,256]{1,0:T(8,128)S(1)}, s32[72,256]{1,0:T(8,128)S(1)}, u32[]{:S(2)}, u32[]{:S(2)}) collective-permute-start(s32[72,256]{1,0:T(8,128)S(1)} %local_message.1.refs_0_), channel_id=1, source_target_pairs={{128,32},{129,33},{130,34},{131,35},{132,36},{133,37},{134,38},{13... | collective-permute-start | bytes 221192 | tf_op jit(solution)/shard_map/ppermute | solution.py:224
  7.7 3.5 %collective-permute-start.10 = (s32[72,256]{1,0:T(8,128)S(1)}, s32[72,256]{1,0:T(8,128)S(1)}, u32[]{:S(2)}, u32[]{:S(2)}) collective-permute-start(s32[72,256]{1,0:T(8,128)S(1)} %local_message.1.refs_0_), channel_id=1, source_target_pairs={{144,32},{145,33},{146,34},{147,35},{148,36},{149,37},{150,38},{15... | collective-permute-start | bytes 221192 | tf_op jit(solution)/shard_map/ppermute | solution.py:224
  8.3 3.5 %collective-permute-start.9 = (s32[72,256]{1,0:T(8,128)S(1)}, s32[72,256]{1,0:T(8,128)S(1)}, u32[]{:S(2)}, u32[]{:S(2)}) collective-permute-start(s32[72,256]{1,0:T(8,128)S(1)} %local_message.1.refs_0_), channel_id=1, source_target_pairs={{0,32},{1,33},{2,34},{3,35},{4,36},{5,37},{6,38},{7,39},{8,40},{9,... | collective-permute-start | bytes 221192 | tf_op jit(solution)/shard_map/ppermute | solution.py:224
  9.0 3.5 %collective-permute-start.8 = (s32[72,256]{1,0:T(8,128)S(1)}, s32[72,256]{1,0:T(8,128)S(1)}, u32[]{:S(2)}, u32[]{:S(2)}) collective-permute-start(s32[72,256]{1,0:T(8,128)S(1)} %local_message.1.refs_0_), channel_id=1, source_target_pairs={{224,32},{225,33},{226,34},{227,35},{228,36},{229,37},{230,38},{23... | collective-permute-start | bytes 221192 | tf_op jit(solution)/shard_map/ppermute | solution.py:224
  9.7 3.5 %collective-permute-start.7 = (s32[72,256]{1,0:T(8,128)S(1)}, s32[72,256]{1,0:T(8,128)S(1)}, u32[]{:S(2)}, u32[]{:S(2)}) collective-permute-start(s32[72,256]{1,0:T(8,128)S(1)} %local_message.1.refs_0_), channel_id=1, source_target_pairs={{208,32},{209,33},{210,34},{211,35},{212,36},{213,37},{214,38},{21... | collective-permute-start | bytes 221192 | tf_op jit(solution)/shard_map/ppermute | solution.py:224
  10.5 3.4 %collective-permute-start.6 = (s32[72,256]{1,0:T(8,128)S(1)}, s32[72,256]{1,0:T(8,128)S(1)}, u32[]{:S(2)}, u32[]{:S(2)}) collective-permute-start(s32[72,256]{1,0:T(8,128)S(1)} %local_message.1.refs_0_), channel_id=1, source_target_pairs={{192,32},{193,33},{194,34},{195,35},{196,36},{197,37},{198,38},{19... | collective-permute-start | bytes 221192 | tf_op jit(solution)/shard_map/ppermute | solution.py:224
  11.2 2.7 %collective-permute-start.5 = (s32[72,256]{1,0:T(8,128)S(1)}, s32[72,256]{1,0:T(8,128)S(1)}, u32[]{:S(2)}, u32[]{:S(2)}) collective-permute-start(s32[72,256]{1,0:T(8,128)S(1)} %local_message.1.refs_0_), channel_id=1, source_target_pairs={{176,32},{177,33},{178,34},{179,35},{180,36},{181,37},{182,38},{18... | collective-permute-start | bytes 221192 | tf_op jit(solution)/shard_map/ppermute | solution.py:224
  11.8 2.1 %collective-permute-start.4 = (s32[72,256]{1,0:T(8,128)S(1)}, s32[72,256]{1,0:T(8,128)S(1)}, u32[]{:S(2)}, u32[]{:S(2)}) collective-permute-start(s32[72,256]{1,0:T(8,128)S(1)} %local_message.1.refs_0_), channel_id=1, source_target_pairs={{160,32},{161,33},{162,34},{163,35},{164,36},{165,37},{166,38},{16... | collective-permute-start | bytes 221192 | tf_op jit(solution)/shard_map/ppermute | solution.py:224
  12.5 1.4 %collective-permute-start.3 = (s32[72,256]{1,0:T(8,128)S(1)}, s32[72,256]{1,0:T(8,128)S(1)}, u32[]{:S(2)}, u32[]{:S(2)}) collective-permute-start(s32[72,256]{1,0:T(8,128)S(1)} %local_message.1.refs_0_), channel_id=1, source_target_pairs={{240,32},{241,33},{242,34},{243,35},{244,36},{245,37},{246,38},{24... | collective-permute-start | bytes 221192 | tf_op jit(solution)/shard_map/ppermute | solution.py:224
  13.2 0.7 collective-permute-start.2
  14.3 0.7 collective-permute-start.13
  15.0 1.3 %collective-permute-start.18 = (bf16[256,128]{1,0:T(8,128)(2,1)S(1)}, bf16[256,128]{1,0:T(8,128)(2,1)S(1)}, u32[]{:S(2)}, u32[]{:S(2)}) collective-permute-start(bf16[256,128]{1,0:T(8,128)(2,1)S(1)} %add.49), channel_id=1, source_target_pairs={{80,192},{81,193},{82,194},{83,195},{84,196},{85,197},{86,198},{87... | collective-permute-start | bytes 196616 | tf_op jit(solution)/shard_map/ppermute | solution.py:224
  15.7 0.7 collective-permute-start.17
  16.4 4.0 %collective-permute-start.19 = (bf16[256,128]{1,0:T(8,128)(2,1)S(1)}, bf16[256,128]{1,0:T(8,128)(2,1)S(1)}, u32[]{:S(2)}, u32[]{:S(2)}) collective-permute-start(bf16[256,128]{1,0:T(8,128)(2,1)S(1)} %add_add_fusion.1), channel_id=1, source_target_pairs={{80,96},{128,160},{192,224},{81,97},{129,161},{193,225},{82,98},{1... | collective-permute-start | bytes 196616 | tf_op jit(solution)/shard_map/ppermute | solution.py:224
  17.1 4.0 %collective-permute-start.14 = (bf16[256,128]{1,0:T(8,128)(2,1)S(1)}, bf16[256,128]{1,0:T(8,128)(2,1)S(1)}, u32[]{:S(2)}, u32[]{:S(2)}) collective-permute-start(bf16[256,128]{1,0:T(8,128)(2,1)S(1)} %finish.1), channel_id=1, source_target_pairs={{32,16},{33,17},{34,18},{35,19},{36,20},{37,21},{38,22},{39,23},{4... | collective-permute-start | bytes 196616 | tf_op jit(solution)/shard_map/ppermute | solution.py:224
  17.7 3.4 %collective-permute-start.12 = (bf16[256,128]{1,0:T(8,128)(2,1)S(1)}, bf16[256,128]{1,0:T(8,128)(2,1)S(1)}, u32[]{:S(2)}, u32[]{:S(2)}) collective-permute-start(bf16[256,128]{1,0:T(8,128)(2,1)S(1)} %finish.1), channel_id=1, source_target_pairs={{32,0},{33,1},{34,2},{35,3},{36,4},{37,5},{38,6},{39,7},{40,8},{41... | collective-permute-start | bytes 196616 | tf_op jit(solution)/shard_map/ppermute | solution.py:224
  18.4 2.7 %collective-permute-start.16 = (bf16[256,128]{1,0:T(8,128)(2,1)S(1)}, bf16[256,128]{1,0:T(8,128)(2,1)S(1)}, u32[]{:S(2)}, u32[]{:S(2)}) collective-permute-start(bf16[256,128]{1,0:T(8,128)(2,1)S(1)} %add.49), channel_id=1, source_target_pairs={{80,64},{81,65},{82,66},{83,67},{84,68},{85,69},{86,70},{87,71},{8... | collective-permute-start | bytes 196616 | tf_op jit(solution)/shard_map/ppermute | solution.py:224
  19.1 61.4 %collective-permute-start.15 = (bf16[256,128]{1,0:T(8,128)(2,1)S(1)}, bf16[256,128]{1,0:T(8,128)(2,1)S(1)}, u32[]{:S(2)}, u32[]{:S(2)}) collective-permute-start(bf16[256,128]{1,0:T(8,128)(2,1)S(1)} %add.49), channel_id=1, source_target_pairs={{80,48},{81,49},{82,50},{83,51},{84,52},{85,53},{86,54},{87,55},{8... | collective-permute-start | bytes 196616 | tf_op jit(solution)/shard_map/ppermute | solution.py:224
  20.4 60.1 %collective-permute-start.20 = (bf16[256,128]{1,0:T(8,128)(2,1)S(1)}, bf16[256,128]{1,0:T(8,128)(2,1)S(1)}, u32[]{:S(2)}, u32[]{:S(2)}) collective-permute-start(bf16[256,128]{1,0:T(8,128)(2,1)S(1)} %add.57), channel_id=1, source_target_pairs={{80,112},{128,144},{160,176},{192,208},{224,240},{81,113},{129,145... | collective-permute-start | bytes 196616 | tf_op jit(solution)/shard_map/ppermute | solution.py:224

commit v3 on v2

--- a/solution.py
+++ b/solution.py
@@ -225,30 +225,41 @@
 
 
 ROOT = 2
-LATE = (15, 10, 11, 12, 13, 14, 0, 9, 8)
-TREE = (((3, 2), (7, 6), (5, 4)), ((1, 2), (6, 4)), ((4, 2),))
+GATHER = (
+    ('in15', 0, ((15, 2),)),
+    ('in10', 0, ((10, 2),)),
+    ('in11', 0, ((11, 2),)),
+    ('in12', 0, ((12, 2),)),
+    ('in13', 0, ((13, 2),)),
+    ('in14', 0, ((14, 2),)),
+    ('in0', 0, ((0, 2),)),
+    ('tree0', 0, ((3, 2), (7, 6), (5, 4), (9, 8))),
+    ('in8', 1, ((8, 2),)),
+    ('tree1', 1, ((1, 2), (6, 4))),
+    ('tree2', 2, ((4, 2),)),
+)
 FAN = (
     ('fan0', (), ((2, 0),)),
-    ('fan1', (), ((2, 5),)),
-    ('fan2', (), ((2, 1),)),
-    ('fan3', ('fan1',), ((5, 3),)),
-    ('fan4', ('fan1',), ((5, 4),)),
-    ('fan5', ('fan1',), ((5, 8),)),
-    ('fan6', ('fan1',), ((5, 12),)),
-    ('fan7', ('fan1', 'fan5', 'fan6'), ((5, 6), (8, 10), (12, 14))),
-    ('fan8', ('fan1', 'fan5', 'fan6', 'fan7'), ((5, 7), (8, 9), (10, 11), (12, 13), (14, 15))),
+    ('fan1', (), ((2, 1),)),
+    ('fan2', (), ((2, 3),)),
+    ('fan3', (), ((2, 5),)),
+    ('fan4', ('fan3',), ((5, 4),)),
+    ('fan5', ('fan3',), ((5, 8),)),
+    ('fan6', ('fan3',), ((5, 12),)),
+    ('fan7', ('fan3', 'fan5', 'fan6'), ((5, 6), (8, 10), (12, 14))),
+    ('fan8', ('fan3', 'fan5', 'fan6', 'fan7'), ((6, 7), (8, 9), (10, 11), (12, 13), (14, 15))),
 )
 
 
 def per_device(q_latent, q_rope, cache_latent, rope_keys, lengths, slot_request, value_up):
-    own = local_message(q_latent, q_rope, cache_latent, rope_keys, lengths, slot_request, value_up)
-    late = [send(own, (z, ROOT)) for z in LATE]
-    near = [own]
-    for i, pairs in enumerate(TREE):
-        if i:
-            near = [merge(*near)]
-        near.append(send(near[0], *pairs))
-    held = finish(ROOT, [*near, *late])
+    mine = local_message(q_latent, q_rope, cache_latent, rope_keys, lengths, slot_request, value_up)
+    level, branches, direct = 0, [], []
+    for name, merges, pairs in GATHER:
+        if merges > level:
+            mine, branches, level = merge(mine, *branches), [], merges
+        came = send(mine, *pairs)
+        (branches if name.startswith("tree") else direct).append(came)
+    held = finish(ROOT, [mine, *branches, *direct])
     got = {}
     for name, needs, pairs in FAN:
         got[name] = send(sum([got[n] for n in needs], held), *pairs)

time: 81.6 us -> 82.2 us (level)
  the two profiles are of different devices: /device:TPU:448 before, /device:TPU:80 now
where the time goes in v3:
time: 82.2 us; the launch traced here: 81.8 us
  waiting for transfers between devices  46.8 us (57%)
  starting transfers between devices  30.5 us (37%)
  Pallas kernels  3.44 us (4%)
    ppermute x20, waiting for transfers between devices, send(): return lax.ppermute(x, 'seq', pairs)  46.8 us
    ppermute x20, starting transfers between devices, send(): return lax.ppermute(x, 'seq', pairs)  30.5 us
    pallas_call x1, Pallas kernels, local_message(): pl.pallas_call(partial_kernel, name='local_message', out_shape=pltpu.VMEM...  2.93 us
  transfers between devices with their start and end apart: 20, of which 1 were waited for; matrix products, arithmetic and copies ran while one was open for 0% of the time, Pallas kernels for 0%

profile of v3, /device:TPU:80, one launch (start us, length us, event | category | flops | bytes accessed | tf_op | source)
XLA Modules:
  0.0 81.8 jit_solution(18067003068620863983)
XLA Ops:
  0.0 2.9 %local_message.1.refs_0_ = s32[72,256]{1,0:T(8,128)S(1)} custom-call(s32[8]{0:T(128)} %lengths_hbm.1, s32[8]{0:T(128)} %slots_hbm.1, bf16[16,2,16,512]{3,2,1,0:T(8,128)(2,1)} %q_lat_hbm.1, bf16[16,2,16,64]{3,2,1,0:T(8,128)(2,1)} %q_rot_hbm.1, bf16[8,128,512]{2,1,0:T(8,128)(2,1)} %cache_hbm.1, bf16[8,64,128]{2,1,0:T(8,128)(2,1)} %rope_hbm.1, ...), custom_call_target="tpu_custom_call" | custom-call | tf_op jit(solution)/shard_map/local_message/pallas_call | solution.py:160
  2.9 0.7 collective-permute-start
  3.6 0.0 collective-permute-done.refs_1_
  3.6 0.1 merge.2.refs_0_
  3.7 0.7 collective-permute-start.1
  4.4 17.2 %collective-permute-start.9 = (s32[72,256]{1,0:T(8,128)S(1)}, s32[72,256]{1,0:T(8,128)S(1)}, u32[]{:S(2)}, u32[]{:S(2)}) collective-permute-start(s32[72,256]{1,0:T(8,128)S(1)} %local_message.1.refs_0_), channel_id=1, source_target_pairs={{0,32},{1,33},{2,34},{3,35},{4,36},{5,37},{6,38},{7,39},{8,40},{9,... | collective-permute-start | bytes 221192 | tf_op jit(solution)/shard_map/ppermute | solution.py:224
  21.6 0.7 collective-permute-start.8
  22.3 0.7 collective-permute-start.7
  23.0 0.7 collective-permute-start.6
  23.7 0.0 collective-permute-done.1.refs_1_
  23.7 0.7 collective-permute-start.5
  24.3 0.1 merge.3.refs_0_
  24.4 0.0 collective-permute-done.9.refs_8_
  24.5 0.7 collective-permute-start.4
  25.1 0.0 collective-permute-done.8.refs_7_
  25.1 0.7 collective-permute-start.3
  25.8 0.0 collective-permute-done.7.refs_6_
  25.8 0.7 collective-permute-start.10
  26.5 0.0 collective-permute-done.6.refs_5_
  26.5 0.7 collective-permute-start.2
  27.2 0.0 collective-permute-done.5.refs_4_
  27.2 0.0 collective-permute-done.4.refs_3_
  27.2 0.0 collective-permute-done.3.refs_2_
  27.2 0.0 collective-permute-done.10.refs_9_
  27.2 0.0 collective-permute-done.2.refs_1_
  27.2 0.3 finish.1
  27.6 0.7 collective-permute-start.14
  28.2 0.0 collective-permute-done.14
  28.3 0.7 collective-permute-start.17
  28.9 0.7 collective-permute-start.16
  29.6 0.0 collective-permute-done.17
  29.6 0.0 collective-permute-done.16
  29.7 0.7 collective-permute-start.18
  30.3 0.7 collective-permute-start.13
  31.0 0.7 collective-permute-start.12
  31.7 1.3 %collective-permute-start.11 = (bf16[256,128]{1,0:T(8,128)(2,1)S(1)}, bf16[256,128]{1,0:T(8,128)(2,1)S(1)}, u32[]{:S(2)}, u32[]{:S(2)}) collective-permute-start(bf16[256,128]{1,0:T(8,128)(2,1)S(1)} %finish.1), channel_id=1, source_target_pairs={{32,0},{33,1},{34,2},{35,3},{36,4},{37,5},{38,6},{39,7},{40,8},{41... | collective-permute-start | bytes 196616 | tf_op jit(solution)/shard_map/ppermute | solution.py:224
  33.0 0.7 collective-permute-start.15
  33.7 0.0 collective-permute-done.18
  33.7 0.7 collective-permute-start.19
  34.4 0.0 collective-permute-done.13
  34.4 0.0 collective-permute-done.12
  34.4 46.7 %collective-permute-done.11 = bf16[256,128]{1,0:T(8,128)(2,1)S(1)} collective-permute-done((bf16[256,128]{1,0:T(8,128)(2,1)S(1)}, bf16[256,128]{1,0:T(8,128)(2,1)S(1)}, u32[]{:S(2)}, u32[]{:S(2)}) %collective-permute-start.11) | collective-permute-done | bytes 65568 | tf_op jit(solution)/shard_map/ppermute | solution.py:224
  81.1 0.0 collective-permute-done.15
  81.1 0.0 collective-permute-done.19
  81.1 0.7 add_add_fusion
  (3 shorter events, 0.1 us)
Async XLA Ops:
  2.9 0.7 collective-permute-start
  3.7 19.9 %collective-permute-start.1 = (s32[72,256]{1,0:T(8,128)S(1)}, s32[72,256]{1,0:T(8,128)S(1)}, u32[]{:S(2)}, u32[]{:S(2)}) collective-permute-start(s32[72,256]{1,0:T(8,128)S(1)} %merge.2.refs_0_), channel_id=1, source_target_pairs={{16,32},{96,64},{17,33},{97,65},{18,34},{98,66},{19,35},{99,67},{2... | collective-permute-start | bytes 221192 | tf_op jit(solution)/shard_map/ppermute | solution.py:224
  4.4 20.1 %collective-permute-start.9 = (s32[72,256]{1,0:T(8,128)S(1)}, s32[72,256]{1,0:T(8,128)S(1)}, u32[]{:S(2)}, u32[]{:S(2)}) collective-permute-start(s32[72,256]{1,0:T(8,128)S(1)} %local_message.1.refs_0_), channel_id=1, source_target_pairs={{0,32},{1,33},{2,34},{3,35},{4,36},{5,37},{6,38},{7,39},{8,40},{9,... | collective-permute-start | bytes 221192 | tf_op jit(solution)/shard_map/ppermute | solution.py:224
  21.6 3.5 %collective-permute-start.8 = (s32[72,256]{1,0:T(8,128)S(1)}, s32[72,256]{1,0:T(8,128)S(1)}, u32[]{:S(2)}, u32[]{:S(2)}) collective-permute-start(s32[72,256]{1,0:T(8,128)S(1)} %local_message.1.refs_0_), channel_id=1, source_target_pairs={{224,32},{225,33},{226,34},{227,35},{228,36},{229,37},{230,38},{23... | collective-permute-start | bytes 221192 | tf_op jit(solution)/shard_map/ppermute | solution.py:224
  22.3 3.5 %collective-permute-start.7 = (s32[72,256]{1,0:T(8,128)S(1)}, s32[72,256]{1,0:T(8,128)S(1)}, u32[]{:S(2)}, u32[]{:S(2)}) collective-permute-start(s32[72,256]{1,0:T(8,128)S(1)} %local_message.1.refs_0_), channel_id=1, source_target_pairs={{208,32},{209,33},{210,34},{211,35},{212,36},{213,37},{214,38},{21... | collective-permute-start | bytes 221192 | tf_op jit(solution)/shard_map/ppermute | solution.py:224
  23.0 3.5 %collective-permute-start.6 = (s32[72,256]{1,0:T(8,128)S(1)}, s32[72,256]{1,0:T(8,128)S(1)}, u32[]{:S(2)}, u32[]{:S(2)}) collective-permute-start(s32[72,256]{1,0:T(8,128)S(1)} %local_message.1.refs_0_), channel_id=1, source_target_pairs={{192,32},{193,33},{194,34},{195,35},{196,36},{197,37},{198,38},{19... | collective-permute-start | bytes 221192 | tf_op jit(solution)/shard_map/ppermute | solution.py:224
  23.7 3.5 %collective-permute-start.5 = (s32[72,256]{1,0:T(8,128)S(1)}, s32[72,256]{1,0:T(8,128)S(1)}, u32[]{:S(2)}, u32[]{:S(2)}) collective-permute-start(s32[72,256]{1,0:T(8,128)S(1)} %local_message.1.refs_0_), channel_id=1, source_target_pairs={{176,32},{177,33},{178,34},{179,35},{180,36},{181,37},{182,38},{18... | collective-permute-start | bytes 221192 | tf_op jit(solution)/shard_map/ppermute | solution.py:224
  24.5 2.7 %collective-permute-start.4 = (s32[72,256]{1,0:T(8,128)S(1)}, s32[72,256]{1,0:T(8,128)S(1)}, u32[]{:S(2)}, u32[]{:S(2)}) collective-permute-start(s32[72,256]{1,0:T(8,128)S(1)} %local_message.1.refs_0_), channel_id=1, source_target_pairs={{160,32},{161,33},{162,34},{163,35},{164,36},{165,37},{166,38},{16... | collective-permute-start | bytes 221192 | tf_op jit(solution)/shard_map/ppermute | solution.py:224
  25.1 2.1 %collective-permute-start.3 = (s32[72,256]{1,0:T(8,128)S(1)}, s32[72,256]{1,0:T(8,128)S(1)}, u32[]{:S(2)}, u32[]{:S(2)}) collective-permute-start(s32[72,256]{1,0:T(8,128)S(1)} %local_message.1.refs_0_), channel_id=1, source_target_pairs={{240,32},{241,33},{242,34},{243,35},{244,36},{245,37},{246,38},{24... | collective-permute-start | bytes 221192 | tf_op jit(solution)/shard_map/ppermute | solution.py:224
  25.8 1.4 %collective-permute-start.10 = (s32[72,256]{1,0:T(8,128)S(1)}, s32[72,256]{1,0:T(8,128)S(1)}, u32[]{:S(2)}, u32[]{:S(2)}) collective-permute-start(s32[72,256]{1,0:T(8,128)S(1)} %merge.2.refs_0_), channel_id=1, source_target_pairs={{128,32},{129,33},{130,34},{131,35},{132,36},{133,37},{134,38},{13... | collective-permute-start | bytes 221192 | tf_op jit(solution)/shard_map/ppermute | solution.py:224
  26.5 0.7 collective-permute-start.2
  27.6 0.7 collective-permute-start.14
  28.3 1.3 %collective-permute-start.17 = (bf16[256,128]{1,0:T(8,128)(2,1)S(1)}, bf16[256,128]{1,0:T(8,128)(2,1)S(1)}, u32[]{:S(2)}, u32[]{:S(2)}) collective-permute-start(bf16[256,128]{1,0:T(8,128)(2,1)S(1)} %add.49), channel_id=1, source_target_pairs={{80,192},{81,193},{82,194},{83,195},{84,196},{85,197},{86,198},{87... | collective-permute-start | bytes 196616 | tf_op jit(solution)/shard_map/ppermute | solution.py:224
  28.9 0.7 collective-permute-start.16
  29.7 4.0 %collective-permute-start.18 = (bf16[256,128]{1,0:T(8,128)(2,1)S(1)}, bf16[256,128]{1,0:T(8,128)(2,1)S(1)}, u32[]{:S(2)}, u32[]{:S(2)}) collective-permute-start(bf16[256,128]{1,0:T(8,128)(2,1)S(1)} %add_add_fusion.1), channel_id=1, source_target_pairs={{80,96},{128,160},{192,224},{81,97},{129,161},{193,225},{82,98},{1... | collective-permute-start | bytes 196616 | tf_op jit(solution)/shard_map/ppermute | solution.py:224
  30.3 4.0 %collective-permute-start.13 = (bf16[256,128]{1,0:T(8,128)(2,1)S(1)}, bf16[256,128]{1,0:T(8,128)(2,1)S(1)}, u32[]{:S(2)}, u32[]{:S(2)}) collective-permute-start(bf16[256,128]{1,0:T(8,128)(2,1)S(1)} %finish.1), channel_id=1, source_target_pairs={{32,48},{33,49},{34,50},{35,51},{36,52},{37,53},{38,54},{39,55},{4... | collective-permute-start | bytes 196616 | tf_op jit(solution)/shard_map/ppermute | solution.py:224
  31.0 3.4 %collective-permute-start.12 = (bf16[256,128]{1,0:T(8,128)(2,1)S(1)}, bf16[256,128]{1,0:T(8,128)(2,1)S(1)}, u32[]{:S(2)}, u32[]{:S(2)}) collective-permute-start(bf16[256,128]{1,0:T(8,128)(2,1)S(1)} %finish.1), channel_id=1, source_target_pairs={{32,16},{33,17},{34,18},{35,19},{36,20},{37,21},{38,22},{39,23},{4... | collective-permute-start | bytes 196616 | tf_op jit(solution)/shard_map/ppermute | solution.py:224
  31.7 49.5 %collective-permute-start.11 = (bf16[256,128]{1,0:T(8,128)(2,1)S(1)}, bf16[256,128]{1,0:T(8,128)(2,1)S(1)}, u32[]{:S(2)}, u32[]{:S(2)}) collective-permute-start(bf16[256,128]{1,0:T(8,128)(2,1)S(1)} %finish.1), channel_id=1, source_target_pairs={{32,0},{33,1},{34,2},{35,3},{36,4},{37,5},{38,6},{39,7},{40,8},{41... | collective-permute-start | bytes 196616 | tf_op jit(solution)/shard_map/ppermute | solution.py:224
  33.0 48.1 %collective-permute-start.15 = (bf16[256,128]{1,0:T(8,128)(2,1)S(1)}, bf16[256,128]{1,0:T(8,128)(2,1)S(1)}, u32[]{:S(2)}, u32[]{:S(2)}) collective-permute-start(bf16[256,128]{1,0:T(8,128)(2,1)S(1)} %add.49), channel_id=1, source_target_pairs={{80,64},{81,65},{82,66},{83,67},{84,68},{85,69},{86,70},{87,71},{8... | collective-permute-start | bytes 196616 | tf_op jit(solution)/shard_map/ppermute | solution.py:224
  33.7 47.4 %collective-permute-start.19 = (bf16[256,128]{1,0:T(8,128)(2,1)S(1)}, bf16[256,128]{1,0:T(8,128)(2,1)S(1)}, u32[]{:S(2)}, u32[]{:S(2)}) collective-permute-start(bf16[256,128]{1,0:T(8,128)(2,1)S(1)} %add.56), channel_id=1, source_target_pairs={{96,112},{128,144},{160,176},{192,208},{224,240},{97,113},{129,145... | collective-permute-start | bytes 196616 | tf_op jit(solution)/shard_map/ppermute | solution.py:224
